TPU v7x, 32 devices: a whole 2x2x4 slice. The times are simulated.
32 devices in a mesh: grp: 2 (over core), tab: 16 (over z, y, x).
Axes of the slice: x: 2, y: 2, z: 4, core: 2. Of those that a mesh axis runs over, the one named last changes fastest.
Arguments:
- sample_ids: int32 [4, 1024, 1024], P(None, ('grp', 'tab')), may hold values from 0 to 1535
- id_weights: bfloat16 [4, 1024, 1024], P(None, ('grp', 'tab')), may hold values from 0.25 to 2
- dense_features: bfloat16 [4, 1024, 128], P(None, ('grp', 'tab')), may hold values from -6 to 6
- click_labels: int32 [4, 1024], P(None, ('grp', 'tab')), may hold values 0 or 1
- table_shards: bfloat16 [128, 1536, 128], P('tab'), may hold values from -1.1953125 to 1.1953125
- slot_table: int32 [128], replicated, may hold values from 0 to 127, each once
- top_weight: bfloat16 [128, 1024], replicated, may hold values from -0.5 to 0.5
- top_bias: float32 [1024], replicated, may hold values from -3 to 3
- out_weight: bfloat16 [1024], replicated, may hold values from -0.1875 to 0.1875
Outputs:
- logits: float32 [4, 1024], P(None, ('grp', 'tab'))
- grad_top: float32 [128, 1024], replicated
- grad_bias: float32 [1024], replicated
Inputs may be any that keep to these rules, and one draw needn't show every extreme that they name: `slot_table`: a permutation: each table stands in exactly one slot.
All inputs are finite; a program needn't handle non-finite values. No bound on the sum of `click_labels` on one device may be relied on, other than what follows from the above.
Results may differ from a plain program's by a relative error of at most 0.0056.
Values may be sent and summed in bfloat16 or wider, within the bound.
A program may use at most 128 MiB of HBM per device.

v0:
```python
import functools
import math

import jax
import jax.numpy as jnp
from jax import lax
from jax.experimental import pallas as pl
from jax.experimental.pallas import tpu as pltpu
from jax.sharding import PartitionSpec as P

HOTS = 8
LANES = 128
loss_scale = 32768.0
NT = (((1,), (1,)), ((), ()))
TN = (((0,), (0,)), ((), ()))


def score_kernel(hots, chunk, x_ref, d_ref, t_ref, o_ref, lo_ref, key_ref, acc_ref):
    slot = pl.program_id(0)
    rows = x_ref.shape[0]
    vocab = t_ref.shape[1]
    blocks = vocab // LANES
    half = x_ref.shape[1] // 2
    slots = half // hots

    @pl.when(slot == 0)
    def _():
        @pl.loop(0, rows // chunk)
        def _(c):
            at = pl.ds(c * chunk, chunk)
            code = x_ref[at, :].astype(jnp.float32)
            lane = lax.broadcasted_iota(jnp.int32, code.shape, 1)
            high = jnp.zeros(code.shape, jnp.int32)
            for k in range(1, blocks):
                high = high + (code >= float(LANES << k)).astype(jnp.int32)
            low = jnp.right_shift(code.astype(jnp.int32), high) & (LANES - 1)
            lo_ref[at, :] = low
            key_ref[at, :] = jnp.where(lane < half, (lane // hots) * blocks + high, -1)
            acc_ref[at, :] = jnp.zeros(code.shape, jnp.float32)

    @pl.loop(0, rows // chunk)
    def _(c):
        at = pl.ds(c * chunk, chunk)
        feats = d_ref[at, :]
        low = lo_ref[at, :]
        key = key_ref[at, :]
        acc = acc_ref[at, :]
        step = 2 * LANES if vocab % (2 * LANES) == 0 else LANES
        for p in range(vocab // step):
            g = lax.dot_general(feats, t_ref[0, p * step : (p + 1) * step, :], NT,
                                preferred_element_type=jnp.float32)
            for q in range(step // LANES):
                a = p * (step // LANES) + q
                part = g[:, q * LANES : (q + 1) * LANES]
                got = jnp.take_along_axis(part, low, axis=1, mode="promise_in_bounds")
                acc = jnp.where(key == slot * blocks + a, got, acc)
        acc_ref[at, :] = acc

    @pl.when(slot == slots - 1)
    def _():
        w = pltpu.roll(x_ref[...].astype(jnp.float32), half, 1)
        lane = lax.broadcasted_iota(jnp.int32, w.shape, 1)
        prod = jnp.where(lane < half, acc_ref[...] * w, 0.0)
        pick_row = lax.broadcasted_iota(jnp.int32, (slots, 2 * half), 0)
        pick_lane = lax.broadcasted_iota(jnp.int32, (slots, 2 * half), 1)
        pick = (pick_lane // hots == pick_row).astype(jnp.float32)
        total = lax.dot_general(pick, prod, NT, preferred_element_type=jnp.float32,
                                precision=lax.Precision.HIGHEST)
        o_ref[...] = (total * (1.0 / math.sqrt(d_ref.shape[1]))).astype(o_ref.dtype)


def slot_scores(x, d, table):
    rows, lanes = x.shape
    slots, vocab, width = table.shape
    hots = lanes // 2 // slots
    chunk = min(256, rows)
    return pl.pallas_call(
        functools.partial(score_kernel, hots, chunk),
        grid=(slots,),
        out_shape=jax.ShapeDtypeStruct((slots, rows), jnp.bfloat16),
        in_specs=[
            pl.BlockSpec((rows, lanes), lambda s: (0, 0)),
            pl.BlockSpec((rows, width), lambda s: (0, 0)),
            pl.BlockSpec((1, vocab, width), lambda s: (s, 0, 0)),
        ],
        out_specs=pl.BlockSpec((slots, rows), lambda s: (0, 0)),
        scratch_shapes=[
            pltpu.VMEM((rows, lanes), jnp.int32),
            pltpu.VMEM((rows, lanes), jnp.int32),
            pltpu.VMEM((rows, lanes), jnp.float32),
        ],
        cost_estimate=pl.CostEstimate(flops=2 * rows * slots * vocab * width, bytes_accessed=4 << 20,
                                      transcendentals=0),
    )(x, d, table)


def top_kernel(count, s_ref, place_ref, label_ref, w_ref, b_ref, o_ref, logit_ref, grad_ref, bias_ref):
    tables = s_ref.shape[0]
    row = lax.broadcasted_iota(jnp.int32, (tables, tables), 0)
    placed = (place_ref[...] == row).astype(jnp.bfloat16)
    scores = jnp.dot(placed, s_ref[...], preferred_element_type=jnp.float32).astype(jnp.bfloat16)
    pre = lax.dot_general(scores, w_ref[...], TN, preferred_element_type=jnp.float32) + b_ref[...]
    gate = jax.nn.sigmoid(pre)
    hidden = (pre * gate).astype(jnp.bfloat16).astype(jnp.float32)
    out = o_ref[...].astype(jnp.float32)
    logit = jnp.sum(hidden * out, axis=1, keepdims=True)
    logit_ref[...] = logit
    delta = (jax.nn.sigmoid(logit) - label_ref[...].astype(jnp.float32)) * (loss_scale / count)
    slope = gate * (1.0 + pre * (1.0 - gate))
    grad = (delta * out * slope).astype(jnp.bfloat16)
    grad_ref[...] = jnp.dot(scores, grad, preferred_element_type=jnp.float32)
    bias_ref[...] = jnp.sum(grad.astype(jnp.float32), axis=0, keepdims=True)


def top_network(count, scores, slot_table, labels, weight, bias, out):
    tables, samples = scores.shape
    hidden = weight.shape[1]
    return pl.pallas_call(
        functools.partial(top_kernel, count),
        out_shape=(
            jax.ShapeDtypeStruct((samples, 1), jnp.float32),
            jax.ShapeDtypeStruct((tables, hidden), jnp.float32),
            jax.ShapeDtypeStruct((1, hidden), jnp.float32),
        ),
    )(scores, slot_table.reshape(1, -1), labels.reshape(-1, 1), weight, bias.reshape(1, -1), out.reshape(1, -1))


def per_device(
    sample_ids, id_weights, dense_features, click_labels, table_shards, slot_table, top_weight, top_bias, out_weight
):
    micro, local_batch, columns = sample_ids.shape
    tables = slot_table.shape[0]
    slots = table_shards.shape[0]
    width = dense_features.shape[2]
    hidden = top_weight.shape[1]
    members = lax.axis_size("tab")
    groups = lax.axis_size("grp")
    samples = micro * local_batch
    count = samples * groups * members
    hots = columns // tables
    own = slots * hots

    ids = sample_ids.reshape(samples, columns)
    power = jnp.left_shift(1, ids // LANES)
    code = ((LANES + ids % LANES) * power).astype(jnp.bfloat16)
    weights = id_weights.reshape(samples, columns)
    source = (slot_table[:, None] * hots + jnp.arange(hots, dtype=jnp.int32)[None, :]).reshape(-1)
    permute = (lax.broadcasted_iota(jnp.int32, (columns, columns), 0) == source[None, :]).astype(jnp.bfloat16)
    both = jnp.dot(jnp.concatenate([code, weights], 0), permute, preferred_element_type=jnp.float32)
    both = both.astype(jnp.bfloat16)
    both = both.reshape(2, samples, members, own).transpose(2, 1, 0, 3).reshape(members * samples, 2 * own)
    x = lax.all_to_all(both, "tab", split_axis=0, concat_axis=0, tiled=True)
    d = lax.all_gather(dense_features.reshape(samples, width), "tab", axis=0, tiled=True)
    mine = slot_scores(x, d, table_shards)
    scores = lax.all_to_all(mine, "tab", split_axis=1, concat_axis=0, tiled=True)
    logit, grad, bias = top_network(
        count, scores, slot_table, click_labels.reshape(samples), top_weight, top_bias, out_weight
    )
    piece = hidden // groups
    blocks = grad.reshape(members, slots, groups, piece).transpose(2, 0, 1, 3)
    got = lax.all_to_all(blocks.reshape(groups * members, slots, piece), ("grp", "tab"), split_axis=0, concat_axis=0,
                         tiled=True)
    part = jnp.sum(got, axis=0)
    whole = lax.all_gather(part, ("grp", "tab"), axis=0, tiled=False)
    grad_top = whole.reshape(groups, members, slots, piece).transpose(1, 2, 0, 3).reshape(tables, hidden)
    bias_all = lax.all_gather(bias, ("grp", "tab"), axis=0, tiled=True)
    grad_bias = jnp.sum(bias_all, axis=0)
    return (logit.reshape(micro, local_batch), grad_top, grad_bias)


def solution(mesh):
    return jax.shard_map(
        per_device,
        mesh=mesh,
        in_specs=(
            P(None, ("grp", "tab"), None),
            P(None, ("grp", "tab"), None),
            P(None, ("grp", "tab"), None),
            P(None, ("grp", "tab")),
            P("tab", None, None),
            P(),
            P(),
            P(),
            P(),
        ),
        out_specs=(P(None, ("grp", "tab")), P(), P()),
        check_vma=False,
    )
```

profile of v0, /device:TPU:0, one launch (start us, length us, event | category | flops | bytes accessed | tf_op | source)
XLA Modules:
  0.0 303.3 jit_solution(5126605743418913812)
XLA Ops:
  0.6 0.7 broadcast_multiply_fusion
  1.3 0.1 iota_add_fusion
  1.4 0.1 add.36
  1.5 1.6 fusion.5
  3.0 0.0 copy-start.1
  3.0 2.0 fusion.2
  5.0 0.2 copy.25
  5.2 0.1 reshape.67
  5.4 0.9 copy.26
  6.3 8.3 %all-to-all-start = ((bf16[16,128,128]{1,2,0:T(8,128)(2,1)}), bf16[16,128,128]{1,2,0:T(8,128)(2,1)S(1)}, u32[]{:S(2)}, u32[]{:S(2)}) async-start(bf16[16,128,128]{1,2,0:T(8,128)(2,1)} %bitcast.3), calls=%async_computation | async-start | bytes 1048576 | tf_op jit(solution)/shard_map/all_to_all | solution.py:152
  14.6 0.0 copy-done.1
  14.6 48.0 %all_gather.12.d_ref = bf16[2048,128]{1,0:T(8,128)(2,1)} all-gather(bf16[128,128]{1,0:T(8,128)(2,1)S(1)} %bitcast.52), channel_id=1, replica_groups=mesh['grp'=2,'tab'=16] {'tab'}, dimensions={0}, use_global_device_ids=true | all-gather | bytes 557056 | tf_op jit(solution)/shard_map/all_gather | solution.py:153
  62.6 0.0 all-to-all-done
  62.6 1.0 copy.27
  63.6 78.9 %shard_map.112 = bf16[8,2048]{1,0:T(8,128)(2,1)} custom-call(bf16[2048,128]{1,0:T(8,128)(2,1)} %bitcast.50, bf16[2048,128]{1,0:T(8,128)(2,1)} %all_gather.12.d_ref, bf16[8,1536,128]{2,1,0:T(8,128)(2,1)} %t_ref.1), custom_call_target="tpu_custom_call" | custom-call | flops 6442450944 | bytes 4194304 | tf_op jit(solution)/shard_map/pallas_call | solution.py:77
  142.5 3.5 %all-to-all-start.1 = ((bf16[8,16,128]{2,0,1:T(8,128)(2,1)}), bf16[8,16,128]{2,0,1:T(8,128)(2,1)S(1)}, u32[]{:S(2)}, u32[]{:S(2)}) async-start(bf16[8,16,128]{2,0,1:T(8,128)(2,1)} %bitcast.53), calls=%async_computation.1 | async-start | bytes 65536 | tf_op jit(solution)/shard_map/all_to_all | solution.py:155
  146.0 0.0 copy-done.2
  146.0 0.7 reshape_reshape.4.label_ref
  146.7 0.6 reshape.71.o_ref
  147.3 6.0 %all-to-all-done.1 = bf16[8,16,128]{2,0,1:T(8,128)(2,1)S(1)} async-done(((bf16[8,16,128]{2,0,1:T(8,128)(2,1)}), bf16[8,16,128]{2,0,1:T(8,128)(2,1)S(1)}, u32[]{:S(2)}, u32[]{:S(2)}) %all-to-all-start.1) | async-done | bytes 32800 | tf_op jit(solution)/shard_map/all_to_all | solution.py:155
  153.3 0.6 copy-done
  154.0 2.7 shard_map.113
  156.6 1.9 copy.29
  158.5 2.6 all-to-all-start.2
  161.1 0.9 reduce.1
  162.0 0.7 reshape.72
  162.7 69.8 %all-gather.1 = f32[32,1,1024]{2,1,0:T(1,128)S(1)} all-gather(f32[1,1,1024]{2,1,0:T(1,128)} %bitcast.55), channel_id=1, replica_groups=mesh['grp'=2,'tab'=16] {'grp','tab'}, dimensions={0}, use_global_device_ids=true | all-gather | bytes 135168 | tf_op jit(solution)/shard_map/all_gather | solution.py:166
  232.5 0.7 reduce_sum.19
  233.2 0.0 all-to-all-done.2
  233.2 68.8 %all-gather = f32[256,512]{1,0:T(8,128)S(1)} all-gather(f32[8,512]{1,0:T(8,128)S(1)} %reduce_sum.18), channel_id=2, replica_groups=mesh['grp'=2,'tab'=16] {'grp','tab'}, dimensions={0}, use_global_device_ids=true | all-gather | bytes 540672 | tf_op jit(solution)/shard_map/all_gather | solution.py:164
  302.0 0.4 copy.33
  302.4 0.9 copy.31
  (5 shorter events, 0.1 us)
Async XLA Ops:
  3.0 11.6 %copy-start.1 = (bf16[4,32,128]{2,1,0:T(8,128)(2,1)S(1)}, bf16[4,32,128]{2,1,0:T(8,128)(2,1)}, u32[]{:S(2)}) copy-start(bf16[4,32,128]{2,1,0:T(8,128)(2,1)} %param.11) | copy-start | bytes 98308
  6.3 56.3 %all-to-all-start = ((bf16[16,128,128]{1,2,0:T(8,128)(2,1)}), bf16[16,128,128]{1,2,0:T(8,128)(2,1)S(1)}, u32[]{:S(2)}, u32[]{:S(2)}) async-start(bf16[16,128,128]{1,2,0:T(8,128)(2,1)} %bitcast.3), calls=%async_computation | async-start | bytes 1048576 | tf_op jit(solution)/shard_map/all_to_all | solution.py:152
  63.6 82.4 %copy-start.2 = (s32[4,32]{1,0:T(4,128)S(1)}, s32[4,32]{1,0:T(4,128)}, u32[]{:S(2)}) copy-start(s32[4,32]{1,0:T(4,128)} %param.12) | copy-start | bytes 1540
  63.6 83.1 %copy-start.3 = (bf16[1024]{0:T(1024)(128)(2,1)S(1)}, bf16[1024]{0:T(1024)(128)(2,1)}, u32[]{:S(2)}) copy-start(bf16[1024]{0:T(1024)(128)(2,1)} %param.17) | copy-start | bytes 6148
  142.5 10.9 %all-to-all-start.1 = ((bf16[8,16,128]{2,0,1:T(8,128)(2,1)}), bf16[8,16,128]{2,0,1:T(8,128)(2,1)S(1)}, u32[]{:S(2)}, u32[]{:S(2)}) async-start(bf16[8,16,128]{2,0,1:T(8,128)(2,1)} %bitcast.53), calls=%async_computation.1 | async-start | bytes 65536 | tf_op jit(solution)/shard_map/all_to_all | solution.py:155
  153.3 0.6 copy-start
  158.5 74.7 %all-to-all-start.2 = ((f32[32,8,512]{2,1,0:T(8,128)}), f32[32,8,512]{2,1,0:T(8,128)S(1)}, u32[]{:S(2)}, u32[]{:S(2)}) async-start(f32[32,8,512]{2,1,0:T(8,128)} %bitcast.13), calls=%async_computation.2 | async-start | bytes 1048576 | tf_op jit(solution)/shard_map/all_to_all | solution.py:161
where the time goes:
time: 304 us; the launch traced here: 303 us
  blocking collectives  187 us (62%)
  Pallas kernels  81.5 us (27%)
  starting transfers between devices  14.4 us (5%)
  local copies, waits for them, and re-layouts  8.13 us (3%)
  waiting for transfers between devices  6.04 us (2%)
  other arithmetic  3.98 us (1%)
    pallas_call x1, Pallas kernels, slot_scores(): pl.pallas_call(functools.partial(score_kernel, hots, chunk), grid=(slots,...  78.9 us
    all_gather x1, blocking collectives, per_device(): bias_all = lax.all_gather(bias, ('grp', 'tab'), axis=0, tiled=True)  69.8 us
    all_gather x1, blocking collectives, per_device(): whole = lax.all_gather(part, ('grp', 'tab'), axis=0, tiled=False)  68.8 us
    all_gather x1, blocking collectives, per_device(): lax.all_gather(dense_features.reshape(samples, width), 'tab', axis=0, til...  48 us
    all_to_all x1, starting transfers between devices, per_device(): x = lax.all_to_all(both, 'tab', split_axis=0, concat_axis=0, tiled=True)  8.35 us
  transfers between devices with their start and end apart: 3, of which 1 were waited for; matrix products, arithmetic and copies ran while one was open for 1% of the time, Pallas kernels for 0%

commit v1 on v0

--- a/solution.py
+++ b/solution.py
@@ -125,6 +125,11 @@
     )(scores, slot_table.reshape(1, -1), labels.reshape(-1, 1), weight, bias.reshape(1, -1), out.reshape(1, -1))
 
 
+def spread(block, axes, count):
+    copies = jnp.broadcast_to(block[None], (count,) + block.shape)
+    return lax.all_to_all(copies, axes, split_axis=0, concat_axis=0, tiled=True)
+
+
 def per_device(
     sample_ids, id_weights, dense_features, click_labels, table_shards, slot_table, top_weight, top_bias, out_weight
 ):
@@ -141,8 +146,8 @@
     own = slots * hots
 
     ids = sample_ids.reshape(samples, columns)
-    power = jnp.left_shift(1, ids // LANES)
-    code = ((LANES + ids % LANES) * power).astype(jnp.bfloat16)
+    power = jnp.left_shift(1, ids >> (LANES.bit_length() - 1))
+    code = ((LANES + (ids & (LANES - 1))) * power).astype(jnp.bfloat16)
     weights = id_weights.reshape(samples, columns)
     source = (slot_table[:, None] * hots + jnp.arange(hots, dtype=jnp.int32)[None, :]).reshape(-1)
     permute = (lax.broadcasted_iota(jnp.int32, (columns, columns), 0) == source[None, :]).astype(jnp.bfloat16)
@@ -150,7 +155,8 @@
     both = both.astype(jnp.bfloat16)
     both = both.reshape(2, samples, members, own).transpose(2, 1, 0, 3).reshape(members * samples, 2 * own)
     x = lax.all_to_all(both, "tab", split_axis=0, concat_axis=0, tiled=True)
-    d = lax.all_gather(dense_features.reshape(samples, width), "tab", axis=0, tiled=True)
+    d = spread(dense_features.reshape(samples, width), "tab", members)
+    d = d.reshape(members * samples, width)
     mine = slot_scores(x, d, table_shards)
     scores = lax.all_to_all(mine, "tab", split_axis=1, concat_axis=0, tiled=True)
     logit, grad, bias = top_network(
@@ -161,10 +167,9 @@
     got = lax.all_to_all(blocks.reshape(groups * members, slots, piece), ("grp", "tab"), split_axis=0, concat_axis=0,
                          tiled=True)
     part = jnp.sum(got, axis=0)
-    whole = lax.all_gather(part, ("grp", "tab"), axis=0, tiled=False)
+    whole = spread(part, ("grp", "tab"), groups * members)
     grad_top = whole.reshape(groups, members, slots, piece).transpose(1, 2, 0, 3).reshape(tables, hidden)
-    bias_all = lax.all_gather(bias, ("grp", "tab"), axis=0, tiled=True)
-    grad_bias = jnp.sum(bias_all, axis=0)
+    grad_bias = jnp.sum(spread(bias.reshape(-1, LANES), ("grp", "tab"), groups * members), axis=0).reshape(hidden)
     return (logit.reshape(micro, local_batch), grad_top, grad_bias)
 
 

time: 304 us -> 196 us (0.64)
  blocking collectives: 187 us -> 41.7 us
  waiting for transfers between devices: 6.04 us -> 42.8 us
    all_gather x3 -> x0, blocking collectives: 187 us -> none  [the longest x1 69.8 us: per_device(): bias_all = lax.all_gather(bias, ('grp', 'tab'), axis=0, tiled=True)]
    all_to_all x0 -> x2, blocking collectives: none -> 41.7 us  [the longest x1 23.2 us: per_device(): x = lax.all_to_all(both, 'tab', split_axis=0, concat_axis=0, tiled=True)]
    all_to_all x2 -> x3, waiting for transfers between devices: 0.01 us -> 36.7 us  [spread(): return lax.all_to_all(copies, axes, split_axis=0, concat_axis=0, tiled=True)]
    broadcast_in_dim x0 -> x3, local copies, waits for them, and re-layouts: none -> 3.1 us  [spread(): copies = jnp.broadcast_to(block[None], (count,) + block.shape)]
    all_to_all x2 -> x3, starting transfers between devices: 11 us -> 9.13 us  [spread(): return lax.all_to_all(copies, axes, split_axis=0, concat_axis=0, tiled=True)]
  transfers between devices with their start and end apart: 3 -> 4, of which waited for: 1 -> 4; matrix products, arithmetic and copies ran while one was open for 1% -> 2% of each run, Pallas kernels for 0% -> 0%
where the time goes in v1:
time: 196 us; the launch traced here: 195 us
  Pallas kernels  81.5 us (42%)
  waiting for transfers between devices  42.8 us (22%)
  blocking collectives  41.7 us (21%)
  starting transfers between devices  13 us (7%)
  local copies, waits for them, and re-layouts  10.5 us (5%)
  other arithmetic  2.67 us (1%)
  matrix products  1.96 us (1%)
    pallas_call x1, Pallas kernels, slot_scores(): pl.pallas_call(functools.partial(score_kernel, hots, chunk), grid=(slots,...  78.9 us
    all_to_all x3, waiting for transfers between devices, spread(): return lax.all_to_all(copies, axes, split_axis=0, concat_axis=0, tiled=True)  36.7 us
    all_to_all x1, blocking collectives, per_device(): x = lax.all_to_all(both, 'tab', split_axis=0, concat_axis=0, tiled=True)  23.2 us
    all_to_all x1, blocking collectives, per_device(): lax.all_to_all(blocks.reshape(groups * members, slots, piece), ('grp', 't...  18.5 us
    all_to_all x3, starting transfers between devices, spread(): return lax.all_to_all(copies, axes, split_axis=0, concat_axis=0, tiled=True)  9.13 us
    all_to_all x1, waiting for transfers between devices, per_device(): lax.all_to_all(mine, 'tab', split_axis=1, concat_axis=0, tiled=True)  6.05 us
  transfers between devices with their start and end apart: 4, of which 4 were waited for; matrix products, arithmetic and copies ran while one was open for 2% of the time, Pallas kernels for 0%

profile of v1, /device:TPU:0, one launch (start us, length us, event | category | flops | bytes accessed | tf_op | source)
XLA Modules:
  0.0 194.9 jit_solution(5354374816121804239)
XLA Ops:
  0.6 1.2 multiply_convert_fusion
  1.8 0.7 broadcast_multiply_fusion
  2.6 2.0 %fusion.2 = bf16[256,1024]{1,0:T(8,128)(2,1)S(1)} fusion(s32[1024]{0:T(1024)S(1)} %add.32, bf16[128,1024]{1,0:T(8,128)(2,1)} %bitcast.45, bf16[128,1024]{1,0:T(8,128)(2,1)S(1)} %bitcast.37), kind=kOutput, calls=%fused_computation.3 | convolution fusion | flops 539230208 | bytes 1052672 | tf_op jit(solution)/shard_map/dot_general | solution.py:154
  4.6 0.2 copy.25
  4.8 0.1 reshape.80
  4.9 0.1 copy.26
  5.1 23.2 %all_to_all.50 = bf16[16,128,128]{1,2,0:T(8,128)(2,1)S(1)} all-to-all(bf16[16,128,128]{1,2,0:T(8,128)(2,1)S(1)} %bitcast.31), channel_id=1, replica_groups=mesh['grp'=2,'tab'=16] {'tab'}, dimensions={0} | all-to-all | bytes 1048576 | tf_op jit(solution)/shard_map/all_to_all | solution.py:157
  28.3 0.9 broadcast_in_dim.11
  29.2 3.9 %all-to-all-start.1 = ((bf16[16,128,128]{2,1,0:T(8,128)(2,1)}), bf16[16,128,128]{2,1,0:T(8,128)(2,1)S(1)}, u32[]{:S(2)}, u32[]{:S(2)}) async-start(bf16[16,128,128]{2,1,0:T(8,128)(2,1)} %broadcast_in_dim.11), calls=%async_computation.1 | async-start | bytes 1048576 | tf_op jit(solution)/shard_map/all_to_all | solution.py:130
  33.1 1.0 copy.27
  34.2 13.4 %all-to-all-done.1 = bf16[16,128,128]{2,1,0:T(8,128)(2,1)S(1)} async-done(((bf16[16,128,128]{2,1,0:T(8,128)(2,1)}), bf16[16,128,128]{2,1,0:T(8,128)(2,1)S(1)}, u32[]{:S(2)}, u32[]{:S(2)}) %all-to-all-start.1) | async-done | bytes 524320 | tf_op jit(solution)/shard_map/all_to_all | solution.py:130
  47.6 0.8 copy-done
  48.4 78.9 %shard_map.112 = bf16[8,2048]{1,0:T(8,128)(2,1)} custom-call(bf16[2048,128]{1,0:T(8,128)(2,1)} %bitcast.35, bf16[2048,128]{1,0:T(8,128)(2,1)} %bitcast.34, bf16[8,1536,128]{2,1,0:T(8,128)(2,1)} %t_ref.1), custom_call_target="tpu_custom_call" | custom-call | flops 6442450944 | bytes 4194304 | tf_op jit(solution)/shard_map/pallas_call | solution.py:77
  127.2 3.9 %all-to-all-start.2 = ((bf16[8,16,128]{2,0,1:T(8,128)(2,1)}), bf16[8,16,128]{2,0,1:T(8,128)(2,1)S(1)}, u32[]{:S(2)}, u32[]{:S(2)}) async-start(bf16[8,16,128]{2,0,1:T(8,128)(2,1)} %bitcast.40), calls=%async_computation.2 | async-start | bytes 65536 | tf_op jit(solution)/shard_map/all_to_all | solution.py:161
  131.1 0.7 reshape_reshape.4.label_ref
  131.9 0.6 reshape.84.o_ref
  132.5 6.1 %all-to-all-done.2 = bf16[8,16,128]{2,0,1:T(8,128)(2,1)S(1)} async-done(((bf16[8,16,128]{2,0,1:T(8,128)(2,1)}), bf16[8,16,128]{2,0,1:T(8,128)(2,1)S(1)}, u32[]{:S(2)}, u32[]{:S(2)}) %all-to-all-start.2) | async-done | bytes 32800 | tf_op jit(solution)/shard_map/all_to_all | solution.py:161
  138.5 0.6 copy-done.1
  139.1 2.7 %shard_map.113 = (f32[128,1]{1,0:T(8,128)}, f32[128,1024]{1,0:T(8,128)}, f32[1,1024]{1,0:T(1,128)}) custom-call(bf16[128,128]{1,0:T(8,128)(2,1)} %bitcast.38, s32[1,128]{1,0:T(1,128)} %bitcast.44, s32[128,1]{1,0:T(8,128)} %reshape_reshape.4.label_ref, bf16[128,1024]{1,0:T(8,128)(2,1)} %w_ref.1, f32[1,1024]{1,0:T(1,128)} %bitcast.41, ...), custom_call_target="tpu_custom_call" | custom-call | tf_op jit(solution)/shard_map/pallas_call | solution.py:118
  141.8 1.1 copy.29
  142.9 18.5 %all_to_all.51 = f32[32,8,512]{2,1,0:T(8,128)S(1)} all-to-all(f32[32,8,512]{2,1,0:T(8,128)S(1)} %bitcast.32), channel_id=1, replica_groups=mesh['grp'=2,'tab'=16] {'grp','tab'}, dimensions={0} | all-to-all | bytes 1048576 | tf_op jit(solution)/shard_map/all_to_all | solution.py:167
  161.4 1.3 broadcast_in_dim.26
  162.8 2.6 %all-to-all-start.5 = ((f32[32,8,128]{2,1,0:T(8,128)}), f32[32,8,128]{2,1,0:T(8,128)S(1)}, u32[]{:S(2)}, u32[]{:S(2)}) async-start(f32[32,8,128]{2,1,0:T(8,128)} %broadcast_in_dim.26), calls=%async_computation.5 | async-start | bytes 262144 | tf_op jit(solution)/shard_map/all_to_all | solution.py:130
  165.4 7.9 %all-to-all-done.5 = f32[32,8,128]{2,1,0:T(8,128)S(1)} async-done(((f32[32,8,128]{2,1,0:T(8,128)}), f32[32,8,128]{2,1,0:T(8,128)S(1)}, u32[]{:S(2)}, u32[]{:S(2)}) %all-to-all-start.5) | async-done | bytes 131104 | tf_op jit(solution)/shard_map/all_to_all | solution.py:130
  173.3 0.9 broadcast_in_dim.24
  174.2 2.6 %all-to-all-start.4 = ((f32[32,8,512]{2,1,0:T(8,128)}), f32[32,8,512]{2,1,0:T(8,128)S(1)}, u32[]{:S(2)}, u32[]{:S(2)}) async-start(f32[32,8,512]{2,1,0:T(8,128)} %broadcast_in_dim.24), calls=%async_computation.4 | async-start | bytes 1048576 | tf_op jit(solution)/shard_map/all_to_all | solution.py:130
  176.8 0.1 reduce
  176.9 0.7 reshape.85
  177.6 0.6 reduce_sum.19
  178.2 15.4 %all-to-all-done.4 = f32[32,8,512]{2,1,0:T(8,128)S(1)} async-done(((f32[32,8,512]{2,1,0:T(8,128)}), f32[32,8,512]{2,1,0:T(8,128)S(1)}, u32[]{:S(2)}, u32[]{:S(2)}) %all-to-all-start.4) | async-done | bytes 524320 | tf_op jit(solution)/shard_map/all_to_all | solution.py:130
  193.6 0.4 copy.33
  194.0 0.9 copy.31
  (13 shorter events, 0.2 us)
Async XLA Ops:
  2.6 25.7 %copy-start.3 = (bf16[4,32,128]{2,1,0:T(8,128)(2,1)S(1)}, bf16[4,32,128]{2,1,0:T(8,128)(2,1)}, u32[]{:S(2)}) copy-start(bf16[4,32,128]{2,1,0:T(8,128)(2,1)} %param.11) | copy-start | bytes 98308
  29.2 18.4 %all-to-all-start.1 = ((bf16[16,128,128]{2,1,0:T(8,128)(2,1)}), bf16[16,128,128]{2,1,0:T(8,128)(2,1)S(1)}, u32[]{:S(2)}, u32[]{:S(2)}) async-start(bf16[16,128,128]{2,1,0:T(8,128)(2,1)} %broadcast_in_dim.11), calls=%async_computation.1 | async-start | bytes 1048576 | tf_op jit(solution)/shard_map/all_to_all | solution.py:130
  47.6 0.8 copy-start
  48.4 82.8 %copy-start.4 = (s32[4,32]{1,0:T(4,128)S(1)}, s32[4,32]{1,0:T(4,128)}, u32[]{:S(2)}) copy-start(s32[4,32]{1,0:T(4,128)} %param.12) | copy-start | bytes 1540
  48.4 83.5 %copy-start.5 = (bf16[1024]{0:T(1024)(128)(2,1)S(1)}, bf16[1024]{0:T(1024)(128)(2,1)}, u32[]{:S(2)}) copy-start(bf16[1024]{0:T(1024)(128)(2,1)} %param.17) | copy-start | bytes 6148
  127.2 11.3 %all-to-all-start.2 = ((bf16[8,16,128]{2,0,1:T(8,128)(2,1)}), bf16[8,16,128]{2,0,1:T(8,128)(2,1)S(1)}, u32[]{:S(2)}, u32[]{:S(2)}) async-start(bf16[8,16,128]{2,0,1:T(8,128)(2,1)} %bitcast.40), calls=%async_computation.2 | async-start | bytes 65536 | tf_op jit(solution)/shard_map/all_to_all | solution.py:161
  138.5 0.6 copy-start.1
  141.8 35.0 %copy-start.2 = (f32[128,1]{1,0:T(8,128)S(1)}, f32[128,1]{1,0:T(8,128)}, u32[]{:S(2)}) copy-start(f32[128,1]{1,0:T(8,128)} %get-tuple-element.6) | copy-start | bytes 1540
  162.8 10.6 %all-to-all-start.5 = ((f32[32,8,128]{2,1,0:T(8,128)}), f32[32,8,128]{2,1,0:T(8,128)S(1)}, u32[]{:S(2)}, u32[]{:S(2)}) async-start(f32[32,8,128]{2,1,0:T(8,128)} %broadcast_in_dim.26), calls=%async_computation.5 | async-start | bytes 262144 | tf_op jit(solution)/shard_map/all_to_all | solution.py:130
  174.2 19.4 %all-to-all-start.4 = ((f32[32,8,512]{2,1,0:T(8,128)}), f32[32,8,512]{2,1,0:T(8,128)S(1)}, u32[]{:S(2)}, u32[]{:S(2)}) async-start(f32[32,8,512]{2,1,0:T(8,128)} %broadcast_in_dim.24), calls=%async_computation.4 | async-start | bytes 1048576 | tf_op jit(solution)/shard_map/all_to_all | solution.py:130

commit v2 on v1

v2 whole, which is shorter than its diff:
```python
import functools
import math

import jax
import jax.numpy as jnp
from jax import lax
from jax.experimental import pallas as pl
from jax.experimental.pallas import tpu as pltpu
from jax.sharding import PartitionSpec as P

HOTS = 8
LANES = 128
loss_scale = 32768.0
NT = (((1,), (1,)), ((), ()))
MESH = pl.DeviceIdType.MESH
TN = (((0,), (0,)), ((), ()))


def score_kernel(hots, chunk, x_ref, d_ref, t_ref, o_ref, lo_ref, key_ref, acc_ref, even_ref, odd_ref):
    slot = pl.program_id(0)
    rows = x_ref.shape[0]
    vocab = t_ref.shape[1]
    blocks = vocab // LANES
    half = x_ref.shape[1] // 2
    slots = half // hots
    chunks = rows // chunk
    group = 8

    @pl.when(slot == 0)
    def _():
        @pl.loop(0, chunks)
        def _(c):
            at = pl.ds(c * chunk, chunk)
            code = x_ref[at, :].astype(jnp.float32)
            lane = lax.broadcasted_iota(jnp.int32, code.shape, 1)
            high = jnp.zeros(code.shape, jnp.int32)
            for k in range(1, blocks):
                high = high + (code >= float(LANES << k)).astype(jnp.int32)
            low = jnp.right_shift(code.astype(jnp.int32), high) & (LANES - 1)
            lo_ref[at, :] = low
            key_ref[at, :] = jnp.where(lane < half, (lane // hots) * blocks + high, -1)
            acc_ref[at, :] = jnp.zeros(code.shape, jnp.float32)

    def multiply(c, g_ref):
        feats = d_ref[pl.ds(pl.multiple_of(c * chunk, chunk), chunk), :]
        step = 2 * LANES if vocab % (2 * LANES) == 0 else LANES
        for p in range(vocab // step):
            g_ref[:, p * step : (p + 1) * step] = lax.dot_general(
                feats, t_ref[0, p * step : (p + 1) * step, :], NT, preferred_element_type=jnp.float32)

    def pick(c, g_ref):
        for r in range(chunk // group):
            at = pl.ds(pl.multiple_of(c * chunk + r * group, group), group)
            low = lo_ref[at, :]
            key = key_ref[at, :] - slot * blocks
            acc = acc_ref[at, :]
            for a in range(blocks):
                part = g_ref[r * group : (r + 1) * group, a * LANES : (a + 1) * LANES]
                got = jnp.take_along_axis(part, low, axis=1, mode="promise_in_bounds")
                acc = jnp.where(key == a, got, acc)
            acc_ref[at, :] = acc

    multiply(0, even_ref)

    @pl.loop(0, chunks // 2)
    def _(i):
        multiply(2 * i + 1, odd_ref)
        pick(2 * i, even_ref)
        multiply(jnp.minimum(2 * i + 2, chunks - 1), even_ref)
        pick(2 * i + 1, odd_ref)

    @pl.when(slot == slots - 1)
    def _():
        w = pltpu.roll(x_ref[...].astype(jnp.float32), half, 1)
        lane = lax.broadcasted_iota(jnp.int32, w.shape, 1)
        prod = jnp.where(lane < half, acc_ref[...] * w, 0.0)
        pick_row = lax.broadcasted_iota(jnp.int32, (slots, 2 * half), 0)
        pick_lane = lax.broadcasted_iota(jnp.int32, (slots, 2 * half), 1)
        choose = (pick_lane // hots == pick_row).astype(jnp.float32)
        total = lax.dot_general(choose, prod, NT, preferred_element_type=jnp.float32,
                                precision=lax.Precision.HIGHEST)
        total = (total * (1.0 / math.sqrt(d_ref.shape[1]))).astype(jnp.bfloat16).astype(jnp.float32)
        samples = o_ref.shape[2]
        for m in range(o_ref.shape[0]):
            o_ref[m] = total[:, m * samples : (m + 1) * samples]


def slot_scores(x, d, table, members):
    rows, lanes = x.shape
    slots, vocab, width = table.shape
    hots = lanes // 2 // slots
    chunk = min(256, rows // 2)
    return pl.pallas_call(
        functools.partial(score_kernel, hots, chunk),
        grid=(slots,),
        out_shape=jax.ShapeDtypeStruct((members, slots, rows // members), jnp.float32),
        in_specs=[
            pl.BlockSpec((rows, lanes), lambda s: (0, 0)),
            pl.BlockSpec((rows, width), lambda s: (0, 0)),
            pl.BlockSpec((1, vocab, width), lambda s: (s, 0, 0)),
        ],
        out_specs=pl.BlockSpec((members, slots, rows // members), lambda s: (0, 0, 0)),
        scratch_shapes=[
            pltpu.VMEM((rows, lanes), jnp.int32),
            pltpu.VMEM((rows, lanes), jnp.int32),
            pltpu.VMEM((rows, lanes), jnp.float32),
            pltpu.VMEM((chunk, vocab), jnp.float32),
            pltpu.VMEM((chunk, vocab), jnp.float32),
        ],
        cost_estimate=pl.CostEstimate(flops=2 * rows * slots * vocab * width, bytes_accessed=4 << 20,
                                      transcendentals=0),
    )(x, d, table)


def column_of(row):
    size = row.shape[1]
    eye = lax.broadcasted_iota(jnp.int32, (size, size), 0) == lax.broadcasted_iota(jnp.int32, (size, size), 1)
    return jnp.sum(jnp.where(eye, row, 0.0), axis=1, keepdims=True)


def row_of(column):
    size = column.shape[0]
    eye = lax.broadcasted_iota(jnp.int32, (size, size), 0) == lax.broadcasted_iota(jnp.int32, (size, size), 1)
    return jnp.sum(jnp.where(eye, column, 0.0), axis=0, keepdims=True)


def top_kernel(count, groups, members, s_ref, place_ref, label_ref, w_ref, b_ref, o_ref,
               logit_ref, top_ref, bias_ref,
               got_ref, grad_ref, slope_ref, part_ref, sum_ref, bias_mine, bias_part,
               send1, recv1, send2, recv2, send3, recv3, send4, recv4):
    my_g, my_t = lax.axis_index("grp"), lax.axis_index("tab")
    total = groups * members
    slots = s_ref.shape[1]
    tables, samples = got_ref.shape
    hidden = w_ref.shape[1]
    piece = hidden // groups
    me = my_g * members + my_t

    def peer(k):
        p = lax.rem(me + k, total)
        return p // members, lax.rem(p, members)

    barrier = pltpu.get_barrier_semaphore()

    @pl.loop(1, total)
    def _(k):
        g, t = peer(k)
        pl.semaphore_signal(barrier, inc=1, device_id={"grp": g, "tab": t}, device_id_type=MESH)

    pl.semaphore_wait(barrier, total - 1)

    def score_copy(k):
        t = lax.rem(my_t + k, members)
        return pltpu.make_async_remote_copy(
            src_ref=s_ref.at[t], dst_ref=got_ref.at[pl.ds(pl.multiple_of(my_t * slots, slots), slots), :],
            send_sem=send1.at[k], recv_sem=recv1.at[k], device_id={"grp": my_g, "tab": t}, device_id_type=MESH)

    @pl.loop(1, members)
    def _(k):
        score_copy(k).start()

    got_ref[pl.ds(pl.multiple_of(my_t * slots, slots), slots), :] = s_ref[my_t]

    @pl.loop(1, members)
    def _(k):
        score_copy(k).wait()

    row = lax.broadcasted_iota(jnp.int32, (tables, tables), 0)
    placed = (place_ref[...] == row).astype(jnp.bfloat16)
    scores = jnp.dot(placed, got_ref[...].astype(jnp.bfloat16), preferred_element_type=jnp.float32)
    scores = scores.astype(jnp.bfloat16)
    pre = lax.dot_general(scores, w_ref[...], TN, preferred_element_type=jnp.float32) + b_ref[...]
    gate = jax.nn.sigmoid(pre)
    value = (pre * gate).astype(jnp.bfloat16).astype(jnp.float32)
    out = o_ref[...].astype(jnp.float32)
    logit = jnp.sum(value * out, axis=1, keepdims=True)
    logit_ref[...] = row_of(logit)
    delta = (jax.nn.sigmoid(logit) - column_of(label_ref[...].astype(jnp.float32))) * (loss_scale / count)
    slope = gate * (1.0 + pre * (1.0 - gate))
    slope_ref[...] = (delta * out * slope).astype(jnp.bfloat16)
    grad = slope_ref[...]
    bias = jnp.sum(grad.astype(jnp.float32), axis=0, keepdims=True)
    for i in range(hidden // LANES):
        bias_mine[i : i + 1, :] = bias[:, i * LANES : (i + 1) * LANES]
    grad_ref[...] = jnp.dot(scores, grad, preferred_element_type=jnp.float32)

    def block(g, t):
        return pl.ds(pl.multiple_of(t * slots, slots), slots), pl.ds(pl.multiple_of(g * piece, LANES), piece)

    def bias_copy(k):
        g, t = peer(k)
        return pltpu.make_async_remote_copy(
            src_ref=bias_mine, dst_ref=bias_part.at[k], send_sem=send2.at[k], recv_sem=recv2.at[k],
            device_id={"grp": g, "tab": t}, device_id_type=MESH)

    def reduce_copy(k):
        g, t = peer(k)
        r, c = block(g, t)
        return pltpu.make_async_remote_copy(
            src_ref=grad_ref.at[r, c], dst_ref=part_ref.at[k], send_sem=send3.at[k], recv_sem=recv3.at[k],
            device_id={"grp": g, "tab": t}, device_id_type=MESH)

    @pl.loop(1, total)
    def _(k):
        reduce_copy(k).start()

    @pl.loop(1, total)
    def _(k):
        bias_copy(k).start()

    r, c = block(my_g, my_t)
    part_ref[0] = grad_ref[r, c]
    bias_part[0] = bias_mine[...]

    @pl.loop(1, total)
    def _(k):
        reduce_copy(k).wait()

    sum_ref[...] = jnp.sum(part_ref[...], axis=0)
    top_ref[r, c] = sum_ref[...]

    def spread_copy(k):
        g, t = peer(k)
        return pltpu.make_async_remote_copy(
            src_ref=sum_ref, dst_ref=top_ref.at[r, c], send_sem=send4.at[k], recv_sem=recv4.at[k],
            device_id={"grp": g, "tab": t}, device_id_type=MESH)

    @pl.loop(1, total)
    def _(k):
        spread_copy(k).start()

    @pl.loop(1, total)
    def _(k):
        bias_copy(k).wait()

    def add(j, acc):
        return acc + bias_part[lax.rem(me - j + total, total)]

    bias_ref[...] = lax.fori_loop(1, total, add, bias_part[me])

    @pl.loop(1, total)
    def _(k):
        spread_copy(k).wait()


def top_network(count, groups, members, scores, slot_table, labels, weight, bias, out):
    slots, samples = scores.shape[1:]
    tables, hidden = weight.shape
    piece = hidden // groups
    total = groups * members
    rows = hidden // LANES
    vmem = pl.BlockSpec(memory_space=pltpu.VMEM)
    return pl.pallas_call(
        functools.partial(top_kernel, count, groups, members),
        out_shape=(
            jax.ShapeDtypeStruct((1, samples), jnp.float32),
            jax.ShapeDtypeStruct((tables, hidden), jnp.float32),
            jax.ShapeDtypeStruct((rows, LANES), jnp.float32),
        ),
        in_specs=[vmem] * 6,
        out_specs=(vmem,) * 3,
        scratch_shapes=[
            pltpu.VMEM((tables, samples), jnp.float32),
            pltpu.VMEM((tables, hidden), jnp.float32),
            pltpu.VMEM((samples, hidden), jnp.bfloat16),
            pltpu.VMEM((total, slots, piece), jnp.float32),
            pltpu.VMEM((slots, piece), jnp.float32),
            pltpu.VMEM((rows, LANES), jnp.float32),
            pltpu.VMEM((total, rows, LANES), jnp.float32),
        ] + [pltpu.SemaphoreType.DMA((members,))] * 2 + [pltpu.SemaphoreType.DMA((total,))] * 6,
        compiler_params=pltpu.CompilerParams(collective_id=1, has_side_effects=True),
    )(scores, slot_table.reshape(1, -1), labels.reshape(1, -1), weight, bias.reshape(1, -1), out.reshape(1, -1))


def spread(block, axes, count):
    copies = jnp.broadcast_to(block[None], (count,) + block.shape)
    return lax.all_to_all(copies, axes, split_axis=0, concat_axis=0, tiled=True)


def per_device(
    sample_ids, id_weights, dense_features, click_labels, table_shards, slot_table, top_weight, top_bias, out_weight
):
    micro, local_batch, columns = sample_ids.shape
    tables = slot_table.shape[0]
    slots = table_shards.shape[0]
    width = dense_features.shape[2]
    hidden = top_weight.shape[1]
    members = lax.axis_size("tab")
    groups = lax.axis_size("grp")
    samples = micro * local_batch
    count = samples * groups * members
    hots = columns // tables
    own = slots * hots

    ids = sample_ids.reshape(samples, columns)
    power = jnp.left_shift(1, ids >> (LANES.bit_length() - 1))
    code = ((LANES + (ids & (LANES - 1))) * power).astype(jnp.bfloat16)
    weights = id_weights.reshape(samples, columns)
    source = (slot_table[:, None] * hots + jnp.arange(hots, dtype=jnp.int32)[None, :]).reshape(-1)
    permute = (lax.broadcasted_iota(jnp.int32, (columns, columns), 0) == source[None, :]).astype(jnp.bfloat16)
    both = jnp.dot(jnp.concatenate([code, weights], 0), permute, preferred_element_type=jnp.float32)
    both = both.astype(jnp.bfloat16)
    both = both.reshape(2, samples, members, own).transpose(2, 1, 0, 3).reshape(members * samples, 2 * own)
    x = lax.all_to_all(both, "tab", split_axis=0, concat_axis=0, tiled=True)
    d = spread(dense_features.reshape(samples, width), "tab", members)
    d = d.reshape(members * samples, width)
    mine = slot_scores(x, d, table_shards, members)
    logit, grad_top, grad_bias = top_network(
        count, groups, members, mine, slot_table, click_labels.reshape(samples), top_weight, top_bias, out_weight
    )
    return (logit.reshape(micro, local_batch), grad_top, grad_bias.reshape(hidden))


def solution(mesh):
    return jax.shard_map(
        per_device,
        mesh=mesh,
        in_specs=(
            P(None, ("grp", "tab"), None),
            P(None, ("grp", "tab"), None),
            P(None, ("grp", "tab"), None),
            P(None, ("grp", "tab")),
            P("tab", None, None),
            P(),
            P(),
            P(),
            P(),
        ),
        out_specs=(P(None, ("grp", "tab")), P(), P()),
        check_vma=False,
    )
```

time: 196 us -> 137 us (0.70)
  waiting for transfers between devices: 42.8 us -> 12.2 us
  blocking collectives: 41.7 us -> 23.2 us
  starting transfers between devices: 13 us -> 3.95 us
    pallas_call x1, Pallas kernels: 78.9 us -> 44.2 us  [slot_scores(): pl.pallas_call(functools.partial(score_kernel, hots, chunk), grid=(slots,...]
    pallas_call x1, Pallas kernels: 2.65 us -> 37.3 us  [top_network(): pl.pallas_call(functools.partial(top_kernel, count, groups, members), out...]
    all_to_all x3 -> x1, waiting for transfers between devices: 36.7 us -> 12.2 us  [spread(): return lax.all_to_all(copies, axes, split_axis=0, concat_axis=0, tiled=True)]
    all_to_all x1 -> x0, blocking collectives: 18.5 us -> none  [per_device(): lax.all_to_all(blocks.reshape(groups * members, slots, piece), ('grp', 't...]
    all_to_all x1 -> x0, waiting for transfers between devices: 6.05 us -> none  [per_device(): lax.all_to_all(mine, 'tab', split_axis=1, concat_axis=0, tiled=True)]
    all_to_all x3 -> x1, starting transfers between devices: 9.13 us -> 3.95 us  [spread(): return lax.all_to_all(copies, axes, split_axis=0, concat_axis=0, tiled=True)]
    all_to_all x1 -> x0, starting transfers between devices: 3.89 us -> none  [per_device(): lax.all_to_all(mine, 'tab', split_axis=1, concat_axis=0, tiled=True)]
    broadcast_in_dim x3 -> x1, local copies, waits for them, and re-layouts: 3.1 us -> 0.9 us  [spread(): copies = jnp.broadcast_to(block[None], (count,) + block.shape)]
  transfers between devices with their start and end apart: 4 -> 1, of which waited for: 4 -> 1; matrix products, arithmetic and copies ran while one was open for 2% -> 2% of each run, Pallas kernels for 0% -> 0%
where the time goes in v2:
time: 137 us; the launch traced here: 135 us
  Pallas kernels  81.4 us (59%)
  blocking collectives  23.2 us (17%)
  waiting for transfers between devices  12.2 us (9%)
  local copies, waits for them, and re-layouts  8.78 us (6%)
  starting transfers between devices  3.95 us (3%)
  other arithmetic  3.19 us (2%)
  matrix products  1.96 us (1%)
    pallas_call x1, Pallas kernels, slot_scores(): pl.pallas_call(functools.partial(score_kernel, hots, chunk), grid=(slots,...  44.2 us
    pallas_call x1, Pallas kernels, top_network(): pl.pallas_call(functools.partial(top_kernel, count, groups, members), out...  37.3 us
    all_to_all x1, blocking collectives, per_device(): x = lax.all_to_all(both, 'tab', split_axis=0, concat_axis=0, tiled=True)  23.2 us
    all_to_all x1, waiting for transfers between devices, spread(): return lax.all_to_all(copies, axes, split_axis=0, concat_axis=0, tiled=True)  12.2 us
    unnamed x10, local copies, waits for them, and re-layouts  3.97 us
    all_to_all x1, starting transfers between devices, spread(): return lax.all_to_all(copies, axes, split_axis=0, concat_axis=0, tiled=True)  3.95 us
  transfers between devices with their start and end apart: 1, of which 1 were waited for; matrix products, arithmetic and copies ran while one was open for 2% of the time, Pallas kernels for 0%

profile of v2, /device:TPU:0, one launch (start us, length us, event | category | flops | bytes accessed | tf_op | source)
XLA Modules:
  0.0 135.5 jit_solution(2670072169199016627)
XLA Ops:
  0.6 1.2 multiply_convert_fusion
  1.8 0.7 broadcast_multiply_fusion
  2.4 0.1 iota_add_fusion
  2.5 0.1 add.32
  2.6 0.0 copy-start.1
  2.6 2.0 %fusion.2 = bf16[256,1024]{1,0:T(8,128)(2,1)S(1)} fusion(s32[1024]{0:T(1024)S(1)} %add.32, bf16[128,1024]{1,0:T(8,128)(2,1)} %bitcast.21, bf16[128,1024]{1,0:T(8,128)(2,1)S(1)} %bitcast.16), kind=kOutput, calls=%fused_computation.3 | convolution fusion | flops 539230208 | bytes 1052672 | tf_op jit(solution)/shard_map/dot_general | solution.py:301
  4.6 0.0 copy-start.2
  4.6 0.0 copy-start.3
  4.6 0.2 copy.13
  4.8 0.1 reshape.63
  5.0 0.1 copy.14
  5.1 23.2 %all_to_all.16 = bf16[16,128,128]{1,2,0:T(8,128)(2,1)S(1)} all-to-all(bf16[16,128,128]{1,2,0:T(8,128)(2,1)S(1)} %bitcast.13), channel_id=1, replica_groups=mesh['grp'=2,'tab'=16] {'tab'}, dimensions={0} | all-to-all | bytes 1048576 | tf_op jit(solution)/shard_map/all_to_all | solution.py:304
  28.3 0.0 copy-done.1
  28.3 0.9 broadcast_in_dim.10
  29.2 3.9 %all-to-all-start.1 = ((bf16[16,128,128]{2,1,0:T(8,128)(2,1)}), bf16[16,128,128]{2,1,0:T(8,128)(2,1)S(1)}, u32[]{:S(2)}, u32[]{:S(2)}) async-start(bf16[16,128,128]{2,1,0:T(8,128)(2,1)} %broadcast_in_dim.10), calls=%async_computation.1 | async-start | bytes 1048576 | tf_op jit(solution)/shard_map/all_to_all | solution.py:277
  33.2 0.0 copy-done.2
  33.2 0.6 reshape.67.o_ref
  33.8 0.0 copy-done.3
  33.8 0.6 reshape_reshape.3.label_ref
  34.4 1.0 copy.15
  35.4 12.2 %all-to-all-done.1 = bf16[16,128,128]{2,1,0:T(8,128)(2,1)S(1)} async-done(((bf16[16,128,128]{2,1,0:T(8,128)(2,1)}), bf16[16,128,128]{2,1,0:T(8,128)(2,1)S(1)}, u32[]{:S(2)}, u32[]{:S(2)}) %all-to-all-start.1) | async-done | bytes 524320 | tf_op jit(solution)/shard_map/all_to_all | solution.py:277
  47.6 0.0 copy-start
  47.6 0.8 copy-done
  48.4 44.2 %shard_map.112.s_ref = f32[16,8,128]{2,1,0:T(8,128)} custom-call(bf16[2048,128]{1,0:T(8,128)(2,1)} %bitcast.15, bf16[2048,128]{1,0:T(8,128)(2,1)} %bitcast.14, bf16[8,1536,128]{2,1,0:T(8,128)(2,1)} %t_ref.1), custom_call_target="tpu_custom_call" | custom-call | flops 6442450944 | bytes 4194304 | tf_op jit(solution)/shard_map/pallas_call | solution.py:93
  92.6 37.3 %shard_map.113 = (f32[1,128]{1,0:T(1,128)}, f32[128,1024]{1,0:T(8,128)}, f32[8,128]{1,0:T(8,128)}) custom-call(f32[16,8,128]{2,1,0:T(8,128)} %shard_map.112.s_ref, s32[1,128]{1,0:T(1,128)} %bitcast.20, s32[1,128]{1,0:T(1,128)} %reshape_reshape.3.label_ref, bf16[128,1024]{1,0:T(8,128)(2,1)} %w_ref.1, f32[1,1024]{1,0:T(1,128)} %bitcast.18, ...), custom_call_target="tpu_custom_call" | custom-call | tf_op jit(solution)/shard_map/pallas_call | solution.py:253
  129.8 0.5 broadcast.17
  130.3 1.3 reduce.3
  131.6 0.7 reshape.68
  132.3 1.9 %copy.18 = f32[128,1024]{1,0:T(8,128)} copy(f32[128,1024]{1,0:T(8,128)} %get-tuple-element.13) | data formatting | bytes 1048576
  134.2 1.3 copy.19
Async XLA Ops:
  2.6 25.7 %copy-start.1 = (bf16[4,32,128]{2,1,0:T(8,128)(2,1)S(1)}, bf16[4,32,128]{2,1,0:T(8,128)(2,1)}, u32[]{:S(2)}) copy-start(bf16[4,32,128]{2,1,0:T(8,128)(2,1)} %param.11) | copy-start | bytes 98308
  4.6 28.6 %copy-start.2 = (bf16[1024]{0:T(1024)(128)(2,1)S(1)}, bf16[1024]{0:T(1024)(128)(2,1)}, u32[]{:S(2)}) copy-start(bf16[1024]{0:T(1024)(128)(2,1)} %param.17) | copy-start | bytes 6148
  4.6 29.2 %copy-start.3 = (s32[4,32]{1,0:T(4,128)S(1)}, s32[4,32]{1,0:T(4,128)}, u32[]{:S(2)}) copy-start(s32[4,32]{1,0:T(4,128)} %param.12) | copy-start | bytes 1540
  29.2 18.4 %all-to-all-start.1 = ((bf16[16,128,128]{2,1,0:T(8,128)(2,1)}), bf16[16,128,128]{2,1,0:T(8,128)(2,1)S(1)}, u32[]{:S(2)}, u32[]{:S(2)}) async-start(bf16[16,128,128]{2,1,0:T(8,128)(2,1)} %broadcast_in_dim.10), calls=%async_computation.1 | async-start | bytes 1048576 | tf_op jit(solution)/shard_map/all_to_all | solution.py:277
  47.6 0.8 copy-start

commit v3 on v1

v3 whole, which is shorter than its diff:
```python
import functools
import math

import jax
import jax.numpy as jnp
from jax import lax
from jax.experimental import pallas as pl
from jax.experimental.pallas import tpu as pltpu
from jax.sharding import PartitionSpec as P

HOTS = 8
LANES = 128
loss_scale = 32768.0
NT = (((1,), (1,)), ((), ()))
MESH = pl.DeviceIdType.MESH
TN = (((0,), (0,)), ((), ()))


def column_of(row):
    size = row.shape[1]
    eye = lax.broadcasted_iota(jnp.int32, (size, size), 0) == lax.broadcasted_iota(jnp.int32, (size, size), 1)
    return jnp.sum(jnp.where(eye, row, 0.0), axis=1, keepdims=True)


def row_of(column):
    size = column.shape[0]
    eye = lax.broadcasted_iota(jnp.int32, (size, size), 0) == lax.broadcasted_iota(jnp.int32, (size, size), 1)
    return jnp.sum(jnp.where(eye, column, 0.0), axis=0, keepdims=True)


def step_kernel(count, groups, members, x_ref, d_ref, t_ref, place_ref, label_ref, w_ref, b_ref, o_ref,
                logit_ref, top_ref, bias_ref,
                xs_ref, ds_ref, lo_ref, key_ref, acc_ref, even_ref, odd_ref, mine_ref,
                got_ref, grad_ref, slope_ref, group_ref, half_ref, part_ref, bias_part,
                x_send, x_recv, d_send, d_recv, s_send, s_recv, g_send, g_recv, p_send, p_recv,
                b_send, b_recv, a_send, a_recv, f_send, f_recv, c_send, c_recv):
    my_g, my_t = lax.axis_index("grp"), lax.axis_index("tab")
    slots, vocab, width = t_ref.shape
    samples = x_ref.shape[1]
    blocks = vocab // LANES
    half = x_ref.shape[2] // 2
    hots = half // slots
    tables = got_ref.shape[0]
    hidden = w_ref.shape[1]
    piece = hidden // groups
    per = 2 if members % 2 == 0 else 1
    chunk = per * samples
    tile = 8

    def member(k):
        return lax.rem(my_t + k, members)

    def origin(k):
        return lax.rem(my_t - k + members, members)

    def team(k):
        return lax.rem(my_g + k, groups)

    def team_origin(k):
        return lax.rem(my_g - k + groups, groups)

    def remote(src, dst, send, recv, g, t):
        return pltpu.make_async_remote_copy(src_ref=src, dst_ref=dst, send_sem=send, recv_sem=recv,
                                            device_id={"grp": g, "tab": t}, device_id_type=MESH)

    def rows_of(t):
        return pl.ds(pl.multiple_of(t * slots, slots), slots)

    def cols_of(g):
        return pl.ds(pl.multiple_of(g * piece, LANES), piece)

    barrier = pltpu.get_barrier_semaphore()

    @pl.loop(1, members)
    def _(k):
        pl.semaphore_signal(barrier, inc=1, device_id={"grp": my_g, "tab": member(k)}, device_id_type=MESH)

    @pl.loop(1, groups)
    def _(k):
        pl.semaphore_signal(barrier, inc=1, device_id={"grp": team(k), "tab": my_t}, device_id_type=MESH)

    pl.semaphore_wait(barrier, members + groups - 2)

    def x_copy(k):
        return remote(x_ref.at[member(k)], xs_ref.at[k], x_send.at[k], x_recv.at[k], my_g, member(k))

    def d_copy(k):
        return remote(d_ref, ds_ref.at[k], d_send.at[k], d_recv.at[k], my_g, member(k))

    def s_copy(k):
        return remote(mine_ref.at[k], got_ref.at[rows_of(my_t), :], s_send.at[k], s_recv.at[k], my_g, origin(k))

    @pl.loop(1, members)
    def _(k):
        d_copy(k).start()
        x_copy(k).start()

    xs_ref[0] = x_ref[my_t]
    ds_ref[0] = d_ref[...]

    pick_row = lax.broadcasted_iota(jnp.int32, (slots, 2 * half), 0)
    pick_lane = lax.broadcasted_iota(jnp.int32, (slots, 2 * half), 1)
    choose = (pick_lane // hots == pick_row).astype(jnp.float32)

    @pl.loop(0, members // per)
    def _(i):
        for e in range(per):
            @pl.when(per * i + e > 0)
            def _():
                d_copy(per * i + e).wait_recv()
                x_copy(per * i + e).wait_recv()

        for e in range(per):
            at = pl.ds(e * samples, samples)
            code = xs_ref[per * i + e].astype(jnp.float32)
            lane = lax.broadcasted_iota(jnp.int32, code.shape, 1)
            high = jnp.zeros(code.shape, jnp.int32)
            for k in range(1, blocks):
                high = high + (code >= float(LANES << k)).astype(jnp.int32)
            lo_ref[at, :] = jnp.right_shift(code.astype(jnp.int32), high) & (LANES - 1)
            key_ref[at, :] = jnp.where(lane < half, (lane // hots) * blocks + high, -1)
            acc_ref[at, :] = jnp.zeros(code.shape, jnp.float32)

        def multiply(slot, g_ref):
            feats = ds_ref[pl.ds(per * i, per)].reshape(chunk, width)
            step = 2 * LANES if vocab % (2 * LANES) == 0 else LANES
            for p in range(vocab // step):
                g_ref[:, p * step : (p + 1) * step] = lax.dot_general(
                    feats, t_ref[slot, p * step : (p + 1) * step, :], NT, preferred_element_type=jnp.float32)

        def pick(slot, g_ref):
            for r in range(chunk // tile):
                at = pl.ds(r * tile, tile)
                low = lo_ref[at, :]
                key = key_ref[at, :] - slot * blocks
                acc = acc_ref[at, :]
                for a in range(blocks):
                    part = g_ref[r * tile : (r + 1) * tile, a * LANES : (a + 1) * LANES]
                    got = jnp.take_along_axis(part, low, axis=1, mode="promise_in_bounds")
                    acc = jnp.where(key == a, got, acc)
                acc_ref[at, :] = acc

        multiply(0, even_ref)

        @pl.loop(0, slots // 2)
        def _(p):
            multiply(2 * p + 1, odd_ref)
            pick(2 * p, even_ref)
            multiply(jnp.minimum(2 * p + 2, slots - 1), even_ref)
            pick(2 * p + 1, odd_ref)

        for e in range(per):
            w = pltpu.roll(xs_ref[per * i + e].astype(jnp.float32), half, 1)
            lane = lax.broadcasted_iota(jnp.int32, w.shape, 1)
            prod = jnp.where(lane < half, acc_ref[e * samples : (e + 1) * samples, :] * w, 0.0)
            total = lax.dot_general(choose, prod, NT, preferred_element_type=jnp.float32,
                                    precision=lax.Precision.HIGHEST)
            mine_ref[per * i + e] = (total * (1.0 / math.sqrt(width))).astype(jnp.bfloat16).astype(jnp.float32)

        for e in range(per):
            @pl.when(per * i + e > 0)
            def _():
                s_copy(per * i + e).start()

    got_ref[rows_of(my_t), :] = mine_ref[0]

    @pl.loop(1, members)
    def _(k):
        d_copy(k).wait_send()
        x_copy(k).wait_send()
        s_copy(k).wait()

    row = lax.broadcasted_iota(jnp.int32, (tables, tables), 0)
    placed = (place_ref[...] == row).astype(jnp.bfloat16)
    scores = jnp.dot(placed, got_ref[...].astype(jnp.bfloat16), preferred_element_type=jnp.float32)
    scores = scores.astype(jnp.bfloat16)
    pre = lax.dot_general(scores, w_ref[...], TN, preferred_element_type=jnp.float32) + b_ref[...]
    gate = jax.nn.sigmoid(pre)
    value = (pre * gate).astype(jnp.bfloat16).astype(jnp.float32)
    out = o_ref[...].astype(jnp.float32)
    logit = jnp.sum(value * out, axis=1, keepdims=True)
    logit_ref[...] = row_of(logit)
    delta = (jax.nn.sigmoid(logit) - column_of(label_ref[...].astype(jnp.float32))) * (loss_scale / count)
    slope = gate * (1.0 + pre * (1.0 - gate))
    slope_ref[...] = (delta * out * slope).astype(jnp.bfloat16)
    grad = slope_ref[...]
    grad_ref[pl.ds(tables, 8), :] = jnp.broadcast_to(
        jnp.sum(grad.astype(jnp.float32), axis=0, keepdims=True), (8, hidden))
    grad_ref[pl.ds(0, tables), :] = jnp.dot(scores, grad, preferred_element_type=jnp.float32)

    def g_copy(k):
        return remote(grad_ref.at[:, cols_of(team(k))], group_ref.at[k], g_send.at[k], g_recv.at[k], team(k), my_t)

    @pl.loop(1, groups)
    def _(k):
        g_copy(k).start()

    half_ref[...] = grad_ref[:, cols_of(my_g)]

    @pl.loop(1, groups)
    def _(k):
        g_copy(k).wait()
        half_ref[...] += group_ref[k]

    def p_copy(k):
        return remote(half_ref.at[rows_of(member(k)), :], part_ref.at[k], p_send.at[k], p_recv.at[k], my_g, member(k))

    def b_copy(k):
        return remote(half_ref.at[pl.ds(tables, 1), :], bias_part.at[k], b_send.at[k], b_recv.at[k], my_g, member(k))

    @pl.loop(1, members)
    def _(k):
        p_copy(k).start()

    @pl.loop(1, members)
    def _(k):
        b_copy(k).start()

    part_ref[0] = half_ref[rows_of(my_t), :]
    bias_part[0] = half_ref[tables : tables + 1, :]

    @pl.loop(1, members)
    def _(k):
        p_copy(k).wait()

    own = (rows_of(my_t), cols_of(my_g))
    top_ref[own] = jnp.sum(part_ref[...], axis=0)

    def a_copy(k):
        return remote(top_ref.at[own], top_ref.at[own], a_send.at[k], a_recv.at[k], my_g, member(k))

    def f_copy(k, j):
        at = (rows_of(origin(k)), cols_of(my_g))
        return remote(top_ref.at[at], top_ref.at[at], f_send.at[j, k], f_recv.at[j, k], team(j), my_t)

    def c_copy(j):
        at = bias_ref.at[:, cols_of(my_g)]
        return remote(at, at, c_send.at[j], c_recv.at[j], team(j), my_t)

    @pl.loop(1, members)
    def _(k):
        a_copy(k).start()

    @pl.loop(1, groups)
    def _(j):
        f_copy(0, j).start()

    @pl.loop(1, members)
    def _(k):
        b_copy(k).wait()

    def add(q, total):
        return total + bias_part[lax.rem(my_t - q + members, members)]

    bias_ref[:, cols_of(my_g)] = lax.fori_loop(1, members, add, bias_part[my_t])

    @pl.loop(1, groups)
    def _(j):
        c_copy(j).start()

    @pl.loop(1, members)
    def _(k):
        a_copy(k).wait_recv()

        @pl.loop(1, groups)
        def _(j):
            f_copy(k, j).start()

    @pl.loop(1, members)
    def _(k):
        a_copy(k).wait_send()

    @pl.loop(1, groups)
    def _(j):
        c_copy(j).wait()

        @pl.loop(0, members)
        def _(k):
            f_copy(k, j).wait()


def fused_step(count, groups, members, x, d, table, slot_table, labels, weight, bias, out):
    samples, width = d.shape
    slots, vocab, _ = table.shape
    tables, hidden = weight.shape
    piece = hidden // groups
    chunk = samples * (2 if members % 2 == 0 else 1)
    lanes = x.shape[2]
    vmem = pl.BlockSpec(memory_space=pltpu.VMEM)
    f32, bf16 = jnp.float32, jnp.bfloat16
    dma = pltpu.SemaphoreType.DMA
    return pl.pallas_call(
        functools.partial(step_kernel, count, groups, members),
        out_shape=(
            jax.ShapeDtypeStruct((1, samples), f32),
            jax.ShapeDtypeStruct((tables, hidden), f32),
            jax.ShapeDtypeStruct((1, hidden), f32),
        ),
        in_specs=[vmem] * 8,
        out_specs=(vmem,) * 3,
        scratch_shapes=[
            pltpu.VMEM((members, samples, lanes), bf16),
            pltpu.VMEM((members, samples, width), bf16),
            pltpu.VMEM((chunk, lanes), jnp.int32),
            pltpu.VMEM((chunk, lanes), jnp.int32),
            pltpu.VMEM((chunk, lanes), f32),
            pltpu.VMEM((chunk, vocab), f32),
            pltpu.VMEM((chunk, vocab), f32),
            pltpu.VMEM((members, slots, samples), f32),
            pltpu.VMEM((tables, samples), f32),
            pltpu.VMEM((tables + 8, hidden), f32),
            pltpu.VMEM((samples, hidden), bf16),
            pltpu.VMEM((groups, tables + 8, piece), f32),
            pltpu.VMEM((tables + 8, piece), f32),
            pltpu.VMEM((members, slots, piece), f32),
            pltpu.VMEM((members, 1, piece), f32),
        ]
        + [dma((members,))] * 6 + [dma((groups,))] * 2 + [dma((members,))] * 6
        + [dma((groups, members))] * 2 + [dma((groups,))] * 2,
        compiler_params=pltpu.CompilerParams(collective_id=1, has_side_effects=True),
    )(x, d, table, slot_table.reshape(1, -1), labels.reshape(1, -1), weight, bias.reshape(1, -1), out.reshape(1, -1))


def per_device(
    sample_ids, id_weights, dense_features, click_labels, table_shards, slot_table, top_weight, top_bias, out_weight
):
    micro, local_batch, columns = sample_ids.shape
    tables = slot_table.shape[0]
    slots = table_shards.shape[0]
    width = dense_features.shape[2]
    hidden = top_weight.shape[1]
    members = lax.axis_size("tab")
    groups = lax.axis_size("grp")
    samples = micro * local_batch
    count = samples * groups * members
    hots = columns // tables
    own = slots * hots

    ids = sample_ids.reshape(samples, columns)
    power = jnp.left_shift(1, ids >> (LANES.bit_length() - 1))
    code = ((LANES + (ids & (LANES - 1))) * power).astype(jnp.bfloat16)
    weights = id_weights.reshape(samples, columns)
    source = (slot_table[:, None] * hots + jnp.arange(hots, dtype=jnp.int32)[None, :]).reshape(-1)
    permute = (lax.broadcasted_iota(jnp.int32, (columns, columns), 0) == source[None, :]).astype(jnp.bfloat16)
    both = jnp.dot(jnp.concatenate([code, weights], 0), permute, preferred_element_type=jnp.float32)
    both = both.astype(jnp.bfloat16)
    both = both.reshape(2, samples, members, own).transpose(2, 1, 0, 3).reshape(members, samples, 2 * own)
    logit, grad_top, grad_bias = fused_step(
        count, groups, members, both, dense_features.reshape(samples, width), table_shards, slot_table,
        click_labels.reshape(samples), top_weight, top_bias, out_weight
    )
    return (logit.reshape(micro, local_batch), grad_top, grad_bias.reshape(hidden))


def solution(mesh):
    return jax.shard_map(
        per_device,
        mesh=mesh,
        in_specs=(
            P(None, ("grp", "tab"), None),
            P(None, ("grp", "tab"), None),
            P(None, ("grp", "tab"), None),
            P(None, ("grp", "tab")),
            P("tab", None, None),
            P(),
            P(),
            P(),
            P(),
        ),
        out_specs=(P(None, ("grp", "tab")), P(), P()),
        check_vma=False,
    )
```

time: 196 us -> 96.2 us (0.49)
  waiting for transfers between devices: 42.8 us -> 0 us
  blocking collectives: 41.7 us -> 0 us
  starting transfers between devices: 13 us -> 0 us
  local copies, waits for them, and re-layouts: 10.5 us -> 7.07 us
    all_to_all x4 -> x0, waiting for transfers between devices: 42.8 us -> none  [the longest x3 36.7 us: spread(): return lax.all_to_all(copies, axes, split_axis=0, concat_axis=0, tiled=True)]
    all_to_all x2 -> x0, blocking collectives: 41.7 us -> none  [the longest x1 23.2 us: per_device(): x = lax.all_to_all(both, 'tab', split_axis=0, concat_axis=0, tiled=True)]
    all_to_all x4 -> x0, starting transfers between devices: 13 us -> none  [the longest x3 9.13 us: spread(): return lax.all_to_all(copies, axes, split_axis=0, concat_axis=0, tiled=True)]
    broadcast_in_dim x3 -> x0, local copies, waits for them, and re-layouts: 3.1 us -> none  [spread(): copies = jnp.broadcast_to(block[None], (count,) + block.shape)]
    pallas_call x2 -> x1, Pallas kernels: 81.5 us -> 82.8 us  [fused_step(): pl.pallas_call(functools.partial(step_kernel, count, groups, members), ou...]
  transfers between devices with their start and end apart: 4 -> 0, of which waited for: 4 -> 0; matrix products, arithmetic and copies ran while one was open for 2% -> 0% of each run, Pallas kernels for 0% -> 0%
where the time goes in v3:
time: 96.2 us; the launch traced here: 95.7 us
  Pallas kernels  82.8 us (86%)
  local copies, waits for them, and re-layouts  7.07 us (7%)
  other arithmetic  3.23 us (3%)
  matrix products  1.96 us (2%)
    pallas_call x1, Pallas kernels, fused_step(): pl.pallas_call(functools.partial(step_kernel, count, groups, members), ou...  82.8 us
    unnamed x6, local copies, waits for them, and re-layouts  3.16 us
    dot_general x1, matrix products, per_device(): jnp.dot(jnp.concatenate([code, weights], 0), permute, preferred_element_t...  1.96 us

profile of v3, /device:TPU:0, one launch (start us, length us, event | category | flops | bytes accessed | tf_op | source)
XLA Modules:
  0.0 95.7 jit_solution(15202140097655227771)
XLA Ops:
  0.6 1.2 %multiply_convert_fusion = bf16[4,32,1024]{2,1,0:T(8,128)(2,1)S(1)} fusion(s32[4,32,1024]{2,1,0:T(8,128)} %param.9), kind=kLoop, calls=%fused_computation.7 | loop fusion | flops 786432 | bytes 786432 | tf_op jit(solution)/shard_map/convert_element_type | solution.py:341
  1.8 0.7 broadcast_multiply_fusion
  2.4 0.1 iota_add_fusion
  2.5 0.1 add.32
  2.6 0.0 copy-start
  2.6 0.0 copy-start.1
  2.7 2.0 %fusion.2 = bf16[256,1024]{1,0:T(8,128)(2,1)S(1)} fusion(s32[1024]{0:T(1024)S(1)} %add.32, bf16[128,1024]{1,0:T(8,128)(2,1)} %bitcast.17, bf16[128,1024]{1,0:T(8,128)(2,1)S(1)} %bitcast.12), kind=kOutput, calls=%fused_computation.3 | convolution fusion | flops 539230208 | bytes 1052672 | tf_op jit(solution)/shard_map/dot_general | solution.py:345
  4.6 0.2 copy.13
  4.8 0.1 reshape.61
  5.0 0.1 copy.14
  5.1 1.0 %copy.15.x_ref = bf16[16,128,128]{2,1,0:T(8,128)(2,1)} copy(bf16[16,128,128]{1,2,0:T(8,128)(2,1)S(1)} %bitcast.11) | data formatting | bytes 1048576 | tf_op jit(solution)/shard_map/reshape | solution.py:347
  6.1 0.0 copy-done
  6.1 0.6 reshape.66.o_ref
  6.7 0.0 copy-done.1
  6.7 0.6 reshape_reshape.3.label_ref
  7.3 82.8 %shard_map.112 = (f32[1,128]{1,0:T(1,128)}, f32[128,1024]{1,0:T(8,128)}, f32[1,1024]{1,0:T(1,128)}) custom-call(bf16[16,128,128]{2,1,0:T(8,128)(2,1)} %copy.15.x_ref, bf16[128,128]{1,0:T(8,128)(2,1)} %bitcast.13, bf16[8,1536,128]{2,1,0:T(8,128)(2,1)} %t_ref.1, s32[1,128]{1,0:T(1,128)} %bitcast.16, s32[1,128]{1,0:T(1,128)} %reshape_reshape.3.label_ref, ...), custom_call_target="tpu_custom_call" | custom-call | tf_op jit(solution)/shard_map/pallas_call | solution.py:292
  90.1 0.5 broadcast.17
  90.6 1.3 %reduce.3 = f32[128]{0:T(128)S(1)} reduce(f32[1,128]{1,0:T(1,128)} %get-tuple-element.6, f32[]{:T(128)} %broadcast.17), dimensions={0}, to_apply=%get-tuple-element.6.reduce_sub_computation.3 | reduce | bytes 1028 | tf_op jit(solution)/shard_map/pallas_call | solution.py:292
  91.9 0.7 reshape.67
  92.6 1.9 %copy.18 = f32[128,1024]{1,0:T(8,128)} copy(f32[128,1024]{1,0:T(8,128)} %get-tuple-element.13) | data formatting | bytes 1048576
  94.5 1.3 %copy.19 = f32[1024]{0:T(1024)} copy(f32[1024]{0:T(1024)} %bitcast.14) | data formatting | bytes 8192
Async XLA Ops:
  2.6 3.5 %copy-start = (bf16[1024]{0:T(1024)(128)(2,1)S(1)}, bf16[1024]{0:T(1024)(128)(2,1)}, u32[]{:S(2)}) copy-start(bf16[1024]{0:T(1024)(128)(2,1)} %param.17) | copy-start | bytes 6148
  2.6 4.1 %copy-start.1 = (s32[4,32]{1,0:T(4,128)S(1)}, s32[4,32]{1,0:T(4,128)}, u32[]{:S(2)}) copy-start(s32[4,32]{1,0:T(4,128)} %param.12) | copy-start | bytes 1540

commit v4 on v3

--- a/solution.py
+++ b/solution.py
@@ -28,9 +28,9 @@
     return jnp.sum(jnp.where(eye, column, 0.0), axis=0, keepdims=True)
 
 
-def step_kernel(count, groups, members, x_ref, d_ref, t_ref, place_ref, label_ref, w_ref, b_ref, o_ref,
+def step_kernel(count, groups, members, id_ref, weight_ref, source_ref, d_ref, t_ref, place_ref, label_ref, w_ref, b_ref, o_ref,
                 logit_ref, top_ref, bias_ref,
-                xs_ref, ds_ref, lo_ref, key_ref, acc_ref, even_ref, odd_ref, mine_ref,
+                x_ref, pair_ref, fin_ref, xs_ref, ds_ref, lo_ref, key_ref, acc_ref, even_ref, odd_ref, mine_ref,
                 got_ref, grad_ref, slope_ref, group_ref, half_ref, part_ref, bias_part,
                 x_send, x_recv, d_send, d_recv, s_send, s_recv, g_send, g_recv, p_send, p_recv,
                 b_send, b_recv, a_send, a_recv, f_send, f_recv, c_send, c_recv):
@@ -79,6 +79,18 @@
     def _(k):
         pl.semaphore_signal(barrier, inc=1, device_id={"grp": team(k), "tab": my_t}, device_id_type=MESH)
 
+    columns = id_ref.shape[2]
+    ids = id_ref[...].reshape(samples, columns)
+    code = jnp.left_shift(LANES + (ids & (LANES - 1)), jnp.right_shift(ids, LANES.bit_length() - 1))
+    pair_ref[:, 0:columns] = code.astype(jnp.float32).astype(jnp.bfloat16)
+    pair_ref[:, columns : 2 * columns] = weight_ref[...].reshape(samples, columns)
+
+    @pl.loop(0, members)
+    def _(m):
+        spot = lax.broadcasted_iota(jnp.int32, (2 * columns, 2 * half), 0)
+        chosen = (spot == source_ref[m]).astype(jnp.float32).astype(jnp.bfloat16)
+        x_ref[m] = jnp.dot(pair_ref[...], chosen, preferred_element_type=jnp.float32).astype(jnp.bfloat16)
+
     pl.semaphore_wait(barrier, members + groups - 2)
 
     def x_copy(k):
@@ -179,8 +191,12 @@
     value = (pre * gate).astype(jnp.bfloat16).astype(jnp.float32)
     out = o_ref[...].astype(jnp.float32)
     logit = jnp.sum(value * out, axis=1, keepdims=True)
-    logit_ref[...] = row_of(logit)
-    delta = (jax.nn.sigmoid(logit) - column_of(label_ref[...].astype(jnp.float32))) * (loss_scale / count)
+    logit_row = row_of(logit)
+    micro, local = logit_ref.shape
+    for m in range(micro):
+        logit_ref[m : m + 1, :] = logit_row[:, m * local : (m + 1) * local]
+    labels = jnp.concatenate([label_ref[m : m + 1, :].astype(jnp.float32) for m in range(micro)], axis=1)
+    delta = (jax.nn.sigmoid(logit) - column_of(labels)) * (loss_scale / count)
     slope = gate * (1.0 + pre * (1.0 - gate))
     slope_ref[...] = (delta * out * slope).astype(jnp.bfloat16)
     grad = slope_ref[...]
@@ -223,15 +239,15 @@
     def _(k):
         p_copy(k).wait()
 
-    own = (rows_of(my_t), cols_of(my_g))
-    top_ref[own] = jnp.sum(part_ref[...], axis=0)
+    fin_ref[my_t, :, cols_of(my_g)] = jnp.sum(part_ref[...], axis=0).astype(jnp.bfloat16)
 
     def a_copy(k):
-        return remote(top_ref.at[own], top_ref.at[own], a_send.at[k], a_recv.at[k], my_g, member(k))
+        at = fin_ref.at[my_t, :, cols_of(my_g)]
+        return remote(at, at, a_send.at[k], a_recv.at[k], my_g, member(k))
 
     def f_copy(k, j):
-        at = (rows_of(origin(k)), cols_of(my_g))
-        return remote(top_ref.at[at], top_ref.at[at], f_send.at[j, k], f_recv.at[j, k], team(j), my_t)
+        at = fin_ref.at[origin(k), :, cols_of(my_g)]
+        return remote(at, at, f_send.at[j, k], f_recv.at[j, k], team(j), my_t)
 
     def c_copy(j):
         at = bias_ref.at[:, cols_of(my_g)]
@@ -278,27 +294,34 @@
         def _(k):
             f_copy(k, j).wait()
 
-
-def fused_step(count, groups, members, x, d, table, slot_table, labels, weight, bias, out):
+    for m in range(members):
+        top_ref[m * slots : (m + 1) * slots, :] = fin_ref[m].astype(jnp.float32)
+
+
+def fused_step(count, groups, members, ids, id_weights, source, d, table, slot_table, labels, weight, bias, out):
     samples, width = d.shape
     slots, vocab, _ = table.shape
     tables, hidden = weight.shape
     piece = hidden // groups
     chunk = samples * (2 if members % 2 == 0 else 1)
-    lanes = x.shape[2]
+    lanes = source.shape[2]
+    columns = ids.shape[2]
     vmem = pl.BlockSpec(memory_space=pltpu.VMEM)
     f32, bf16 = jnp.float32, jnp.bfloat16
     dma = pltpu.SemaphoreType.DMA
     return pl.pallas_call(
         functools.partial(step_kernel, count, groups, members),
         out_shape=(
-            jax.ShapeDtypeStruct((1, samples), f32),
+            jax.ShapeDtypeStruct(labels.shape, f32),
             jax.ShapeDtypeStruct((tables, hidden), f32),
             jax.ShapeDtypeStruct((1, hidden), f32),
         ),
-        in_specs=[vmem] * 8,
+        in_specs=[vmem] * 10,
         out_specs=(vmem,) * 3,
         scratch_shapes=[
+            pltpu.VMEM((members, samples, lanes), bf16),
+            pltpu.VMEM((samples, 2 * columns), bf16),
+            pltpu.VMEM((members, slots, hidden), bf16),
             pltpu.VMEM((members, samples, lanes), bf16),
             pltpu.VMEM((members, samples, width), bf16),
             pltpu.VMEM((chunk, lanes), jnp.int32),
@@ -318,7 +341,7 @@
         + [dma((members,))] * 6 + [dma((groups,))] * 2 + [dma((members,))] * 6
         + [dma((groups, members))] * 2 + [dma((groups,))] * 2,
         compiler_params=pltpu.CompilerParams(collective_id=1, has_side_effects=True),
-    )(x, d, table, slot_table.reshape(1, -1), labels.reshape(1, -1), weight, bias.reshape(1, -1), out.reshape(1, -1))
+    )(ids, id_weights, source, d, table, slot_table.reshape(1, -1), labels, weight, bias.reshape(1, -1), out.reshape(1, -1))
 
 
 def per_device(
@@ -336,20 +359,14 @@
     hots = columns // tables
     own = slots * hots
 
-    ids = sample_ids.reshape(samples, columns)
-    power = jnp.left_shift(1, ids >> (LANES.bit_length() - 1))
-    code = ((LANES + (ids & (LANES - 1))) * power).astype(jnp.bfloat16)
-    weights = id_weights.reshape(samples, columns)
-    source = (slot_table[:, None] * hots + jnp.arange(hots, dtype=jnp.int32)[None, :]).reshape(-1)
-    permute = (lax.broadcasted_iota(jnp.int32, (columns, columns), 0) == source[None, :]).astype(jnp.bfloat16)
-    both = jnp.dot(jnp.concatenate([code, weights], 0), permute, preferred_element_type=jnp.float32)
-    both = both.astype(jnp.bfloat16)
-    both = both.reshape(2, samples, members, own).transpose(2, 1, 0, 3).reshape(members, samples, 2 * own)
+    source = slot_table.reshape(members, slots, 1) * hots + jnp.arange(hots, dtype=jnp.int32)
+    source = source.reshape(members, 1, own)
+    source = jnp.concatenate([source, source + columns], axis=2)
     logit, grad_top, grad_bias = fused_step(
-        count, groups, members, both, dense_features.reshape(samples, width), table_shards, slot_table,
-        click_labels.reshape(samples), top_weight, top_bias, out_weight
+        count, groups, members, sample_ids, id_weights, source, dense_features.reshape(samples, width), table_shards,
+        slot_table, click_labels, top_weight, top_bias, out_weight
     )
-    return (logit.reshape(micro, local_batch), grad_top, grad_bias.reshape(hidden))
+    return (logit, grad_top, grad_bias.reshape(hidden))
 
 
 def solution(mesh):

time: 96.2 us -> 93.3 us (0.970)
  Pallas kernels: 82.8 us -> 85 us
  matrix products: 1.96 us -> 0 us
  other arithmetic: 3.23 us -> 1.38 us
  local copies, waits for them, and re-layouts: 7.07 us -> 5.99 us
    pallas_call x1, Pallas kernels: 82.8 us -> 85 us  [fused_step(): pl.pallas_call(functools.partial(step_kernel, count, groups, members), ou...]
    dot_general x1 -> x0, matrix products: 1.96 us -> none  [per_device(): jnp.dot(jnp.concatenate([code, weights], 0), permute, preferred_element_t...]
    reshape x3 -> x0, local copies, waits for them, and re-layouts: 1.8 us -> none  [the longest x2 1.14 us: per_device(): both.reshape(2, samples, members, own).transpose(2, 1, 0, 3)]
    pallas_call x1 -> x0, other arithmetic: 1.33 us -> none  [fused_step(): pl.pallas_call(functools.partial(step_kernel, count, groups, members), ou...]
    unnamed x6 -> x3, local copies, waits for them, and re-layouts: 3.16 us -> 4.4 us
    convert_element_type x1 -> x0, other arithmetic: 1.16 us -> none  [per_device(): code = ((LANES + (ids & LANES - 1)) * power).astype(jnp.bfloat16)]
where the time goes in v4:
time: 93.3 us; the launch traced here: 93 us
  Pallas kernels  85 us (91%)
  local copies, waits for them, and re-layouts  5.99 us (6%)
  other arithmetic  1.38 us (1%)
    pallas_call x1, Pallas kernels, fused_step(): pl.pallas_call(functools.partial(step_kernel, count, groups, members), ou...  85 us
    unnamed x3, local copies, waits for them, and re-layouts  4.4 us

profile of v4, /device:TPU:0, one launch (start us, length us, event | category | flops | bytes accessed | tf_op | source)
XLA Modules:
  0.0 93.0 jit_solution(8470765204147871370)
XLA Ops:
  0.6 0.7 broadcast_multiply_fusion
  1.3 1.3 %reshape.108.o_ref = bf16[1,1024]{1,0:T(2,128)(2,1)} reshape(bf16[1024]{0:T(1024)(128)(2,1)} %param.17) | data formatting | bytes 4096 | tf_op jit(solution)/shard_map/reshape | solution.py:344
  2.6 0.1 add.48
  2.7 0.1 mul.16
  2.7 0.1 copy.14
  2.8 0.1 copy.15
  2.9 0.7 pad_add_fusion.source_ref
  3.6 85.0 %shard_map.112 = (f32[4,32]{1,0:T(4,128)}, f32[128,1024]{1,0:T(8,128)}, f32[1,1024]{1,0:T(1,128)}) custom-call(s32[4,32,1024]{2,1,0:T(8,128)} %id_ref.1, bf16[4,32,1024]{2,1,0:T(8,128)(2,1)} %weight_ref.1, s32[16,1,128]{2,1,0:T(1,128)} %pad_add_fusion.source_ref, bf16[128,128]{1,0:T(8,128)(2,1)} %bitcast.7, bf16[8,1536,128]{2,1,0:T(8,128)(2,1)} %t_ref.1, ...), custom_call_target="tpu_custom_call" | custom-call | tf_op jit(solution)/shard_map/pallas_call | solution.py:312
  88.6 1.2 %copy.20 = f32[4,32]{1,0:T(4,128)} copy(f32[4,32]{1,0:T(4,128)} %get-tuple-element.14) | data formatting | bytes 1024
  89.9 1.9 %copy.21 = f32[128,1024]{1,0:T(8,128)} copy(f32[128,1024]{1,0:T(8,128)} %get-tuple-element.15) | data formatting | bytes 1048576
  91.7 1.3 %copy.22 = f32[1024]{0:T(1024)} copy(f32[1024]{0:T(1024)} %bitcast.9) | data formatting | bytes 8192
  (4 shorter events, 0.0 us)

commit v5 on v4

--- a/solution.py
+++ b/solution.py
@@ -30,7 +30,7 @@
 
 def step_kernel(count, groups, members, id_ref, weight_ref, source_ref, d_ref, t_ref, place_ref, label_ref, w_ref, b_ref, o_ref,
                 logit_ref, top_ref, bias_ref,
-                x_ref, pair_ref, fin_ref, xs_ref, ds_ref, lo_ref, key_ref, acc_ref, even_ref, odd_ref, mine_ref,
+                turned_ref, x_ref, pair_ref, fin_ref, xs_ref, ds_ref, lo_ref, key_ref, acc_ref, even_ref, odd_ref, mine_ref,
                 got_ref, grad_ref, slope_ref, group_ref, half_ref, part_ref, bias_part,
                 x_send, x_recv, d_send, d_recv, s_send, s_recv, g_send, g_recv, p_send, p_recv,
                 b_send, b_recv, a_send, a_recv, f_send, f_recv, c_send, c_recv):
@@ -110,6 +110,10 @@
     xs_ref[0] = x_ref[my_t]
     ds_ref[0] = d_ref[...]
 
+    @pl.loop(0, slots)
+    def _(slot):
+        turned_ref[slot] = t_ref[slot].T
+
     pick_row = lax.broadcasted_iota(jnp.int32, (slots, 2 * half), 0)
     pick_lane = lax.broadcasted_iota(jnp.int32, (slots, 2 * half), 1)
     choose = (pick_lane // hots == pick_row).astype(jnp.float32)
@@ -137,8 +141,8 @@
             feats = ds_ref[pl.ds(per * i, per)].reshape(chunk, width)
             step = 2 * LANES if vocab % (2 * LANES) == 0 else LANES
             for p in range(vocab // step):
-                g_ref[:, p * step : (p + 1) * step] = lax.dot_general(
-                    feats, t_ref[slot, p * step : (p + 1) * step, :], NT, preferred_element_type=jnp.float32)
+                g_ref[:, p * step : (p + 1) * step] = jnp.dot(
+                    feats, turned_ref[slot, :, p * step : (p + 1) * step], preferred_element_type=jnp.float32)
 
         def pick(slot, g_ref):
             for r in range(chunk // tile):
@@ -319,6 +323,7 @@
         in_specs=[vmem] * 10,
         out_specs=(vmem,) * 3,
         scratch_shapes=[
+            pltpu.VMEM((slots, width, vocab), bf16),
             pltpu.VMEM((members, samples, lanes), bf16),
             pltpu.VMEM((samples, 2 * columns), bf16),
             pltpu.VMEM((members, slots, hidden), bf16),

time: 93.3 us -> 93.1 us (level)
  no operation moved by 1% of the time
where the time goes in v5:
time: 93.1 us; the launch traced here: 92.8 us
  Pallas kernels  84.8 us (91%)
  local copies, waits for them, and re-layouts  5.99 us (6%)
  other arithmetic  1.38 us (1%)
    pallas_call x1, Pallas kernels, fused_step(): pl.pallas_call(functools.partial(step_kernel, count, groups, members), ou...  84.8 us
    unnamed x3, local copies, waits for them, and re-layouts  4.4 us

profile of v5, /device:TPU:0, one launch (start us, length us, event | category | flops | bytes accessed | tf_op | source)
XLA Modules:
  0.0 92.8 jit_solution(1920211019410053029)
XLA Ops:
  0.6 0.7 broadcast_multiply_fusion
  1.3 1.3 %reshape.108.o_ref = bf16[1,1024]{1,0:T(2,128)(2,1)} reshape(bf16[1024]{0:T(1024)(128)(2,1)} %param.17) | data formatting | bytes 4096 | tf_op jit(solution)/shard_map/reshape | solution.py:349
  2.6 0.1 add.48
  2.7 0.1 mul.16
  2.7 0.1 copy.14
  2.8 0.1 copy.15
  2.9 0.7 pad_add_fusion.source_ref
  3.6 84.8 %shard_map.112 = (f32[4,32]{1,0:T(4,128)}, f32[128,1024]{1,0:T(8,128)}, f32[1,1024]{1,0:T(1,128)}) custom-call(s32[4,32,1024]{2,1,0:T(8,128)} %id_ref.1, bf16[4,32,1024]{2,1,0:T(8,128)(2,1)} %weight_ref.1, s32[16,1,128]{2,1,0:T(1,128)} %pad_add_fusion.source_ref, bf16[128,128]{1,0:T(8,128)(2,1)} %bitcast.7, bf16[8,1536,128]{2,1,0:T(8,128)(2,1)} %t_ref.1, ...), custom_call_target="tpu_custom_call" | custom-call | tf_op jit(solution)/shard_map/pallas_call | solution.py:316
  88.4 1.2 %copy.20 = f32[4,32]{1,0:T(4,128)} copy(f32[4,32]{1,0:T(4,128)} %get-tuple-element.14) | data formatting | bytes 1024
  89.7 1.9 %copy.21 = f32[128,1024]{1,0:T(8,128)} copy(f32[128,1024]{1,0:T(8,128)} %get-tuple-element.15) | data formatting | bytes 1048576
  91.6 1.3 %copy.22 = f32[1024]{0:T(1024)} copy(f32[1024]{0:T(1024)} %bitcast.9) | data formatting | bytes 8192
  (4 shorter events, 0.0 us)
